TPU v7x, 32 devices: a whole 2x2x4 slice. The times are simulated.
32 devices in a mesh: grp: 16 (over z, y, x), loc: 2 (over core).
Axes of the slice: x: 2, y: 2, z: 4, core: 2. Of those that a mesh axis runs over, the one named last changes fastest.
Arguments:
- tokens: bfloat16 [1024, 3584], P(('grp', 'loc')), may hold values from -6 to 6
- gate_weights: bfloat16 [1024, 8], P(('grp', 'loc')), may hold values from 0.099609375 to 0.59765625
- expert_ids: int32 [1024, 8], P(('grp', 'loc')), may hold values from 0 to 31, as said below
- w_gate: bfloat16 [32, 3584, 1024], P('grp', None, 'loc'), may hold values from -0.09375 to 0.09375
- w_up: bfloat16 [32, 3584, 1024], P('grp', None, 'loc'), may hold values from -0.09375 to 0.09375
- w_down: bfloat16 [32, 3584, 1024], P('grp', None, 'loc'), may hold values from -0.1875 to 0.1875
Outputs:
- layer_out: bfloat16 [1024, 3584], P(('grp', 'loc'))
Inputs may be any that keep to these rules, and one draw needn't show every extreme that they name: `expert_ids`: each row names 8 different experts: two in each of 4 different routing groups, a routing group being 4 consecutive expert numbers. Among the rows of one device (aligned blocks of 32 rows) each expert is named at most 16 times, and in every such block some expert is named exactly 16 times.
All inputs are finite; a program needn't handle non-finite values.
Results may differ from a plain program's by a relative error of at most 0.01.
Values may be sent and summed in bfloat16 or wider, within the bound.
A program may use at most 192 MiB of HBM per device.

v0:
```python
import jax
import jax.numpy as jnp
from jax import lax
from jax.sharding import PartitionSpec as P

RGROUPS = 8


def expert_rows(inputs, scales, gate_part, up_part, down_part):
    gate_act = jnp.dot(inputs, gate_part, preferred_element_type=jnp.float32)
    upward = jnp.dot(inputs, up_part, preferred_element_type=jnp.float32)
    hidden = (jax.nn.silu(gate_act) * upward).astype(jnp.bfloat16)
    projected = lax.dot_general(
        hidden, down_part, (((1,), (1,)), ((), ())), preferred_element_type=jnp.float32
    )
    return projected * scales.astype(jnp.float32)[:, None]


def weights_path(rows_in, scales_in, w_gate, w_up, w_down):
    row_dims = rows_in.shape
    shard_units = w_gate.shape[2]
    expert_inputs = [rows_in[:, expert].reshape(-1, row_dims[3]) for expert in range(row_dims[1])]
    expert_scales = [scales_in[:, expert].reshape(-1) for expert in range(row_dims[1])]
    starting = tuple(
        (
            jnp.zeros((row_dims[0] * row_dims[2], row_dims[3]), jnp.float32)
            for expert in range(row_dims[1])
        )
    )
    gate_piece = lax.all_gather(w_gate, "loc", axis=2, tiled=True)
    up_piece = lax.all_gather(w_up, "loc", axis=2, tiled=True)
    down_piece = lax.all_gather(w_down, "loc", axis=2, tiled=True)
    updated = []
    for expert in range(row_dims[1]):
        running = starting[expert]
        for block_index in range(gate_piece.shape[2] // shard_units):
            lower_unit = block_index * shard_units
            upper_unit = lower_unit + shard_units
            values = expert_rows(
                expert_inputs[expert],
                expert_scales[expert],
                gate_piece[expert][:, lower_unit:upper_unit],
                up_piece[expert][:, lower_unit:upper_unit],
                down_piece[expert][:, lower_unit:upper_unit],
            )
            rounded = lax.optimization_barrier(values.astype(jnp.bfloat16))
            running = running + rounded.astype(jnp.float32)
        updated.append(running)
    folded = tuple(updated)
    stacked = jnp.stack(
        [folded_part.reshape(row_dims[0], row_dims[2], row_dims[3]) for folded_part in folded],
        axis=1,
    )
    return stacked.astype(jnp.bfloat16)


def body(tokens, gate_weights, expert_ids, w_gate, w_up, w_down):
    tok_count = tokens.shape[0]
    choices_per = expert_ids.shape[1]
    feature_count = tokens.shape[1]
    group_count = lax.axis_size("grp")
    local_experts = w_gate.shape[0]
    expert_total = group_count * local_experts
    slot_depth = 2 * tok_count * RGROUPS // expert_total
    slot_total = expert_total * slot_depth
    pair_ids = expert_ids.reshape(-1)
    pair_count = pair_ids.shape[0]
    pair_order = jnp.arange(pair_count, dtype=jnp.int32)
    same_expert = (pair_ids[:, None] == pair_ids[None, :]).astype(jnp.int32)
    earlier = (pair_order[:, None] > pair_order[None, :]).astype(jnp.int32)
    slot_rank = jnp.sum(same_expert * earlier, axis=1)
    position = pair_ids * slot_depth + slot_rank
    pair_onehot = jnp.arange(slot_total, dtype=jnp.int32)[:, None] == position[None, :]
    placement = jnp.sum(
        pair_onehot.reshape(slot_total, tok_count, choices_per).astype(jnp.int32), axis=2
    ).astype(jnp.bfloat16)
    send_rows = jnp.dot(placement, tokens, preferred_element_type=jnp.float32).astype(jnp.bfloat16)
    flat_scales = gate_weights.reshape(-1).astype(jnp.float32)
    send_scales = jnp.sum(jnp.where(pair_onehot, flat_scales[None, :], 0.0), axis=1).astype(
        jnp.bfloat16
    )
    send_rows = send_rows.reshape(group_count, local_experts, slot_depth, feature_count)
    send_scales = send_scales.reshape(group_count, local_experts, slot_depth)
    computed = weights_path(
        lax.all_to_all(send_rows, "grp", split_axis=0, concat_axis=0, tiled=True),
        lax.all_to_all(send_scales, "grp", split_axis=0, concat_axis=0, tiled=True),
        w_gate,
        w_up,
        w_down,
    )
    returned = lax.all_to_all(computed, "grp", split_axis=0, concat_axis=0, tiled=True)
    flat_back = returned.reshape(slot_total, feature_count)
    mixed_out = lax.dot_general(
        placement, flat_back, (((0,), (0,)), ((), ())), preferred_element_type=jnp.float32
    )
    return mixed_out.astype(jnp.bfloat16)


def solution(mesh):
    placed = (
        P(("grp", "loc"), None),
        P(("grp", "loc"), None),
        P(("grp", "loc"), None),
        P("grp", None, "loc"),
        P("grp", None, "loc"),
        P("grp", None, "loc"),
    )
    return jax.shard_map(
        body, mesh=mesh, in_specs=placed, out_specs=P(("grp", "loc"), None), check_vma=False
    )
```

profile of v0, /device:TPU:0, one launch (start us, length us, event | category | flops | bytes accessed | tf_op | source)
XLA Modules:
  0.0 275.2 jit_solution(6262012617588769095)
XLA Ops:
  6.5 0.7 all-gather.4.cloned.1.call-update
  7.3 0.7 all-gather.6.cloned.1.call-update
  8.1 0.7 all-gather.8.cloned.1.call-update
  9.5 0.7 convert_element_type.100
  10.2 8.3 %all-to-all-start.1 = ((bf16[16,2,16]{2,1,0:T(2,128)(2,1)}), bf16[16,2,16]{2,1,0:T(2,128)(2,1)S(1)}, u32[]{:S(2)}, u32[]{:S(2)}) async-start(bf16[16,2,16]{2,1,0:T(2,128)(2,1)} %convert_element_type.100), calls=%async_computation.1 | async-start | bytes 16384 | tf_op jit(solution)/shard_map/all_to_all | solution.py:86
  18.9 3.8 %convolution_convert_fusion = bf16[512,3584]{1,0:T(8,128)(2,1)} fusion(bf16[32,3584]{1,0:T(8,128)(2,1)S(1)} %copy-done, s32[512,32]{0,1:T(8,128)S(1)} %convert_reduce_fusion), kind=kOutput, calls=%fused_computation.6 | convolution fusion | flops 119291904 | bytes 3964928 | tf_op jit(solution)/shard_map/dot_general | solution.py:77
  22.6 3.1 %all-to-all-done.1 = bf16[16,2,16]{2,1,0:T(2,128)(2,1)S(1)} async-done(((bf16[16,2,16]{2,1,0:T(2,128)(2,1)}), bf16[16,2,16]{2,1,0:T(2,128)(2,1)S(1)}, u32[]{:S(2)}, u32[]{:S(2)}) %all-to-all-start.1) | async-done | bytes 1056 | tf_op jit(solution)/shard_map/all_to_all | solution.py:86
  25.7 4.6 %all-to-all-start = ((bf16[16,2,16,3584]{3,2,1,0:T(8,128)(2,1)}), bf16[16,2,16,3584]{3,2,1,0:T(8,128)(2,1)}, u32[]{:S(2)}, u32[]{:S(2)}) async-start(bf16[16,2,16,3584]{3,2,1,0:T(8,128)(2,1)} %bitcast.32), calls=%async_computation | async-start | bytes 7340032 | tf_op jit(solution)/shard_map/all_to_all | solution.py:85
  30.6 69.3 %all-to-all-done = bf16[16,2,16,3584]{3,2,1,0:T(8,128)(2,1)} async-done(((bf16[16,2,16,3584]{3,2,1,0:T(8,128)(2,1)}), bf16[16,2,16,3584]{3,2,1,0:T(8,128)(2,1)}, u32[]{:S(2)}, u32[]{:S(2)}) %all-to-all-start) | async-done | bytes 3670048 | tf_op jit(solution)/shard_map/all_to_all | solution.py:85
  99.9 3.5 %fusion.88 = (bf16[16,1,16,3584]{3,2,1,0:T(8,128)(2,1)}, bf16[16,1,16,3584]{3,2,1,0:T(8,128)(2,1)S(1)}) fusion(bf16[16,2,16,3584]{3,2,1,0:T(8,128)(2,1)} %all-to-all-done), kind=kLoop, calls=%fused_computation.89 | loop fusion | bytes 7340032 | tf_op jit(solution)/shard_map/slice | solution.py:22
  103.4 6.3 %slice_bitcast_fusion.5 = (bf16[3584,1024]{1,0:T(8,128)(2,1)S(1)}, bf16[3584,1024]{1,0:T(8,128)(2,1)S(1)}) fusion(bf16[2,3584,1024]{2,1,0:T(8,128)(2,1)} %all-gather.4.cloned.1.call-done), kind=kLoop, calls=%fused_computation.5 | loop fusion | bytes 29360128 | tf_op jit(solution)/shard_map/squeeze | solution.py:42
  109.7 1.1 fusion.7
  110.8 1.1 fusion.12
  112.3 1.9 fusion.17
  114.3 1.9 fusion.22
  116.2 10.6 %slice_bitcast_fusion.4 = (bf16[3584,1024]{1,0:T(8,128)(2,1)}, bf16[3584,1024]{1,0:T(8,128)(2,1)}) fusion(bf16[2,3584,1024]{2,1,0:T(8,128)(2,1)} %all-gather.6.cloned.1.call-done), kind=kLoop, calls=%fused_computation.4 | loop fusion | bytes 29360128 | tf_op jit(solution)/shard_map/squeeze | solution.py:43
  126.8 10.5 %slice_bitcast_fusion.3 = (bf16[3584,1024]{1,0:T(8,128)(2,1)}, bf16[3584,1024]{1,0:T(8,128)(2,1)}) fusion(bf16[2,3584,1024]{2,1,0:T(8,128)(2,1)} %all-gather.8.cloned.1.call-done), kind=kLoop, calls=%fused_computation.3 | loop fusion | bytes 29360128 | tf_op jit(solution)/shard_map/squeeze | solution.py:44
  137.3 7.4 %fusion = bf16[256,3584]{1,0:T(8,128)(2,1)} fusion(bf16[3584,1024]{1,0:T(8,128)(2,1)} %get-tuple-element.11, f32[256]{0:T(256)S(1)} %reshape.55, bf16[256,3584]{1,0:T(8,128)(2,1)} %bitcast.40, bf16[3584,1024]{1,0:T(8,128)(2,1)} %get-tuple-element.9, f32[256,512]{1,0:T(8,128)} %fusion.22), kind=kOutput, calls=%fused_computation.11 | convolution fusion | flops 1881669632 | bytes 11535360 | tf_op jit(solution)/shard_map/dot_general | solution.py:13
  144.6 7.3 %fusion.1 = bf16[256,3584]{1,0:T(8,128)(2,1)} fusion(bf16[3584,1024]{1,0:T(8,128)(2,1)} %get-tuple-element.11, f32[256]{0:T(256)S(1)} %reshape.55, bf16[256,3584]{1,0:T(8,128)(2,1)} %bitcast.41, bf16[3584,1024]{1,0:T(8,128)(2,1)} %get-tuple-element.9, f32[256,512]{1,0:T(8,128)} %fusion.17), kind=kOutput, calls=%fused_computation.12 | convolution fusion | flops 1881669632 | bytes 11535360 | tf_op jit(solution)/shard_map/dot_general | solution.py:13
  152.0 6.6 %fusion.2 = bf16[256,3584]{1,0:T(8,128)(2,1)} fusion(bf16[3584,1024]{1,0:T(8,128)(2,1)} %get-tuple-element.12, f32[256]{0:T(256)S(1)} %reshape.56, bf16[256,3584]{1,0:T(8,128)(2,1)S(1)} %bitcast.38, bf16[3584,1024]{1,0:T(8,128)(2,1)} %get-tuple-element.10, f32[256,512]{1,0:T(8,128)S(1)} %fusion.12), kind=kOutput, calls=%fused_computation.13 | convolution fusion | flops 1881669632 | bytes 11535360 | tf_op jit(solution)/shard_map/dot_general | solution.py:13
  158.6 6.7 %fusion.3 = bf16[256,3584]{1,0:T(8,128)(2,1)} fusion(bf16[3584,1024]{1,0:T(8,128)(2,1)} %get-tuple-element.12, f32[256]{0:T(256)S(1)} %reshape.56, bf16[256,3584]{1,0:T(8,128)(2,1)S(1)} %bitcast.39, bf16[3584,1024]{1,0:T(8,128)(2,1)} %get-tuple-element.10, f32[256,512]{1,0:T(8,128)S(1)} %fusion.7), kind=kOutput, calls=%fused_computation.14 | convolution fusion | flops 1881669632 | bytes 11535360 | tf_op jit(solution)/shard_map/dot_general | solution.py:13
  165.3 2.6 add_convert_fusion.1
  169.2 98.0 %all_to_all.15 = bf16[16,2,16,3584]{3,2,1,0:T(8,128)(2,1)S(1)} all-to-all(bf16[16,2,16,3584]{3,2,1,0:T(8,128)(2,1)S(1)} %pad_maximum_fusion), channel_id=1, replica_groups=mesh['grp'=16,'loc'=2] {'grp'}, dimensions={0} | all-to-all | bytes 7340032 | tf_op jit(solution)/shard_map/all_to_all | solution.py:91
  267.2 1.4 convolution_convert_fusion.1
  (35 shorter events, 3.0 us)
Async XLA Ops:
  6.5 12.3 %copy-start = (bf16[32,3584]{1,0:T(8,128)(2,1)S(1)}, bf16[32,3584]{1,0:T(8,128)(2,1)}, u32[]{:S(2)}) copy-start(bf16[32,3584]{1,0:T(8,128)(2,1)} %param.6) | copy-start | bytes 688132
  6.5 96.8 %all-gather.4.cloned.1.call-start = ((), (), s32[]{:S(2)}) async-start(), calls=%async_computation.3 | async-start | bytes 22020096 | tf_op jit(solution)/shard_map/all_gather | solution.py:30
  7.3 108.9 %all-gather.6.cloned.1.call-start = ((), (), s32[]{:S(2)}) async-start(), calls=%async_computation.4 | async-start | bytes 22020096 | tf_op jit(solution)/shard_map/all_gather | solution.py:31
  8.0 0.8 copy-start.5
  8.0 0.9 copy-start.6
  8.0 118.7 %all-gather.8.cloned.1.call-start = ((), (), s32[]{:S(2)}) async-start(), calls=%async_computation.5 | async-start | bytes 22020096 | tf_op jit(solution)/shard_map/all_gather | solution.py:32
  10.2 15.6 %all-to-all-start.1 = ((bf16[16,2,16]{2,1,0:T(2,128)(2,1)}), bf16[16,2,16]{2,1,0:T(2,128)(2,1)S(1)}, u32[]{:S(2)}, u32[]{:S(2)}) async-start(bf16[16,2,16]{2,1,0:T(2,128)(2,1)} %convert_element_type.100), calls=%async_computation.1 | async-start | bytes 16384 | tf_op jit(solution)/shard_map/all_to_all | solution.py:86
  25.7 74.1 %all-to-all-start = ((bf16[16,2,16,3584]{3,2,1,0:T(8,128)(2,1)}), bf16[16,2,16,3584]{3,2,1,0:T(8,128)(2,1)}, u32[]{:S(2)}, u32[]{:S(2)}) async-start(bf16[16,2,16,3584]{3,2,1,0:T(8,128)(2,1)} %bitcast.32), calls=%async_computation | async-start | bytes 7340032 | tf_op jit(solution)/shard_map/all_to_all | solution.py:85
  110.8 1.5 copy-start.2
  165.3 2.6 copy-start.3
  165.3 3.2 %copy-start.4 = (bf16[256,3584]{1,0:T(8,128)(2,1)S(1)}, bf16[256,3584]{1,0:T(8,128)(2,1)}, u32[]{:S(2)}) copy-start(bf16[256,3584]{1,0:T(8,128)(2,1)} %fusion.3) | copy-start | bytes 5505028
  169.2 99.4 %copy-start.1 = (bf16[32,3584]{1,0:T(8,128)(2,1)S(1)}, bf16[32,3584]{1,0:T(8,128)(2,1)}, u32[]{:S(2)}) copy-start(bf16[32,3584]{1,0:T(8,128)(2,1)} %param.6) | copy-start | bytes 688132
Sparse Core Ops, SparseCore 0:
  8.9 29.7 all-gather.3
  40.2 28.1 all-gather.5
  70.0 28.1 all-gather.7
where the time goes:
time: 275 us
  blocking collectives  98 us (36%)
  waiting for transfers between devices  74.5 us (27%)
  matrix products  39.3 us (14%)
  local copies, waits for them, and re-layouts  33.1 us (12%)
  between operations  13.3 us (5%)
  starting transfers between devices  13 us (5%)
  other arithmetic  4.04 us (1%)
    all_to_all x1, blocking collectives, body(): lax.all_to_all(computed, 'grp', split_axis=0, concat_axis=0, tiled=True)  98 us
    all_to_all x1, waiting for transfers between devices, body(): lax.all_to_all(send_rows, 'grp', split_axis=0, concat_axis=0, tiled=True)  69.3 us
    dot_general x4, matrix products, expert_rows(): lax.dot_general(hidden, down_part, (((1,), (1,)), ((), ())), preferred_el...  28 us
    squeeze x1, local copies, waits for them, and re-layouts, weights_path(): up_piece[expert][:, lower_unit:upper_unit]  10.6 us
    squeeze x1, local copies, waits for them, and re-layouts, weights_path(): down_piece[expert][:, lower_unit:upper_unit]  10.5 us
    all_to_all x1, starting transfers between devices, body(): lax.all_to_all(send_scales, 'grp', split_axis=0, concat_axis=0, tiled=True)  8.34 us
    squeeze x1, local copies, waits for them, and re-layouts, weights_path(): gate_piece[expert][:, lower_unit:upper_unit]  6.32 us
    dot_general x4, matrix products, expert_rows(): gate_act = jnp.dot(inputs, gate_part, preferred_element_type=jnp.float32)  6.07 us
  transfers between devices with their start and end apart: 5, of which 2 were waited for; matrix products, arithmetic and copies ran while one was open for 12% of the time, Pallas kernels for 0%

commit v1 on v0

--- a/solution.py
+++ b/solution.py
@@ -1,9 +1,312 @@
+import functools
+
 import jax
 import jax.numpy as jnp
 from jax import lax
+from jax.experimental import pallas as pl
+from jax.experimental.pallas import tpu as pltpu
 from jax.sharding import PartitionSpec as P
 
 RGROUPS = 8
+LANES = 128
+MESH = pl.DeviceIdType.MESH
+
+
+class Place:
+    def __init__(self, columns):
+        self.deep = columns // 4
+        self.g = lax.axis_index("grp")
+        self.c = lax.axis_index("loc")
+        self.x = lax.rem(self.g, 2)
+        self.y = lax.rem(lax.div(self.g, 2), 2)
+        self.z = lax.div(self.g, 4)
+        self.below = self.z > 0
+        self.above = self.z < self.deep - 1
+
+    def at(self, dz=0, fx=0, fy=0):
+        x = 1 - self.x if fx else self.x
+        y = 1 - self.y if fy else self.y
+        return (self.z + dz) * 4 + y * 2 + x
+
+    def line(self, step):
+        if step == 0:
+            return [(0, None)]
+        return [(-step, self.z >= step), (step, self.z + step < self.deep)]
+
+
+def when(cond, act):
+    if cond is None:
+        act()
+    else:
+        pl.when(cond)(act)
+
+
+def greet(me):
+    barrier = pltpu.get_barrier_semaphore()
+    partners = [
+        (None, me.at(fx=1), me.c),
+        (None, me.at(fy=1), me.c),
+        (None, me.g, 1 - me.c),
+        (me.below, me.at(dz=-1), me.c),
+        (me.above, me.at(dz=1), me.c),
+    ]
+    for cond, g, c in partners:
+        when(cond, lambda g=g, c=c: pl.semaphore_signal(
+            barrier, inc=1, device_id=(g, c), device_id_type=MESH))
+    edges = (me.z > 0).astype(jnp.int32) + (me.z < me.deep - 1).astype(jnp.int32)
+    pl.semaphore_wait(barrier, 3 + edges)
+
+
+def gather_kernel(columns, own_ref, out_ref, own_sem, send_sem, ici_sem, loc_sem):
+    me = Place(columns)
+    rows = own_ref.shape[0]
+    half = rows // 2
+    greet(me)
+
+    def slot(h, g, c):
+        return out_ref.at[pl.ds(pl.multiple_of((g * 2 + c) * rows + h * half, half), half)]
+
+    base = pl.multiple_of((me.g * 2 + me.c) * rows, rows)
+    keep = pltpu.make_async_copy(own_ref, out_ref.at[pl.ds(base, rows)], own_sem)
+    keep.start()
+    sends = []
+
+    def push(cond, h, g, kind, device, own):
+        source = own_ref.at[pl.ds(h * half, half)] if own else slot(h, g, me.c)
+        arrive = loc_sem if kind == 4 else ici_sem
+        copy = pltpu.make_async_remote_copy(
+            src_ref=source, dst_ref=slot(h, g, me.c),
+            send_sem=send_sem.at[h, g, kind], recv_sem=arrive.at[h, g],
+            device_id=device, device_id_type=MESH)
+        when(cond, copy.start)
+        sends.append((cond, copy))
+
+    def arrived(cond, h, g):
+        copy = pltpu.make_async_remote_copy(
+            src_ref=slot(h, g, me.c), dst_ref=slot(h, g, me.c),
+            send_sem=send_sem.at[h, g, 0], recv_sem=ici_sem.at[h, g],
+            device_id=(me.g, 1 - me.c), device_id_type=MESH)
+        when(cond, copy.wait_recv)
+
+    def both(a, b):
+        return b if a is None else jnp.logical_and(a, b)
+
+    flips = [dict(fx=1), dict(fy=1)]
+
+    def first(step):
+        for dz, cond in me.line(step):
+            for h in range(2):
+                g = me.at(dz)
+                if step:
+                    arrived(cond, h, g)
+                if dz <= 0:
+                    push(both(cond, me.above), h, g, 0, (me.at(1), me.c), step == 0)
+                if dz >= 0:
+                    push(both(cond, me.below), h, g, 1, (me.at(-1), me.c), step == 0)
+                push(cond, h, g, 2, (me.at(**flips[h]), me.c), step == 0)
+                push(cond, h, g, 3, (me.at(**flips[1 - h]), me.c), step == 0)
+                push(cond, h, g, 4, (me.g, 1 - me.c), step == 0)
+
+    def second(step):
+        for dz, cond in me.line(step):
+            for h in range(2):
+                g = me.at(dz, **flips[h])
+                arrived(cond, h, g)
+                push(cond, h, g, 3, (me.at(**flips[1 - h]), me.c), False)
+                push(cond, h, g, 4, (me.g, 1 - me.c), False)
+
+    def third(step):
+        for dz, cond in me.line(step):
+            for h in range(2):
+                for g in (me.at(dz, **flips[1 - h]), me.at(dz, fx=1, fy=1)):
+                    arrived(cond, h, g)
+                    push(cond, h, g, 4, (me.g, 1 - me.c), False)
+
+    for turn in range(me.deep + 2):
+        for stage, lag in ((first, 0), (second, 1), (third, 2)):
+            if 0 <= turn - lag < me.deep:
+                stage(turn - lag)
+    for h in range(2):
+        for g in range(columns):
+            pltpu.make_async_remote_copy(
+                src_ref=slot(h, g, 1 - me.c), dst_ref=slot(h, g, 1 - me.c),
+                send_sem=send_sem.at[h, g, 4], recv_sem=loc_sem.at[h, g],
+                device_id=(me.g, 1 - me.c), device_id_type=MESH).wait_recv()
+    for cond, copy in sends:
+        when(cond, copy.wait_send)
+    keep.wait()
+
+
+def gather_tokens(joined, columns):
+    rows, width = joined.shape
+    dma = pltpu.SemaphoreType.DMA
+    return pl.pallas_call(
+        functools.partial(gather_kernel, columns),
+        out_shape=jax.ShapeDtypeStruct((columns * 2 * rows, width), joined.dtype),
+        in_specs=[pl.BlockSpec(memory_space=pltpu.VMEM)],
+        out_specs=pl.BlockSpec(memory_space=pltpu.VMEM),
+        scratch_shapes=[dma, dma((2, columns, 5)), dma((2, columns)), dma((2, columns))],
+        compiler_params=pltpu.CompilerParams(
+            collective_id=1, has_side_effects=True, vmem_limit_bytes=24 * 2**20),
+        name="gather_tokens",
+    )(joined)
+
+
+def scatter_kernel(columns, part_ref, out_ref, sums, from_loc, from_two, from_one, from_low,
+                   from_high, loc_send, send_sem, loc_sem, two_sem, one_sem, low_sem, high_sem):
+    me = Place(columns)
+    rows = out_ref.shape[0]
+    half = rows // 2
+    width = out_ref.shape[1]
+    piece = width // 4 if width % (4 * LANES) == 0 else width
+    greet(me)
+    flips = [dict(fx=1), dict(fy=1)]
+    sends = []
+
+    def start(h, g):
+        return pl.multiple_of((g * 2 + me.c) * rows + h * half, half)
+
+    def to_core(h, g, cond):
+        base = pl.multiple_of((g * 2 + 1 - me.c) * rows + h * half, half)
+        copy = pltpu.make_async_remote_copy(
+            src_ref=part_ref.at[pl.ds(base, half)], dst_ref=from_loc.at[h, g],
+            send_sem=loc_send.at[h, g], recv_sem=loc_sem.at[h, g],
+            device_id=(me.g, 1 - me.c), device_id_type=MESH)
+        when(cond, copy.start)
+        sends.append((cond, copy))
+
+    def send(cond, h, g, buffer, sem, device):
+        copy = pltpu.make_async_remote_copy(
+            src_ref=sums.at[h, g], dst_ref=buffer.at[h, g],
+            send_sem=send_sem.at[h, g], recv_sem=sem.at[h, g],
+            device_id=device, device_id_type=MESH)
+        when(cond, copy.start)
+        sends.append((cond, copy))
+
+    def add(h, g, terms, final=False):
+        for buffer, sem in terms:
+            pltpu.make_async_remote_copy(
+                src_ref=buffer.at[h, g], dst_ref=buffer.at[h, g],
+                send_sem=send_sem.at[h, g], recv_sem=sem.at[h, g],
+                device_id=(me.g, 1 - me.c), device_id_type=MESH).wait_recv()
+        for low in range(0, width, piece):
+            cols = slice(low, low + piece)
+            total = part_ref[pl.ds(start(h, g), half), cols].astype(jnp.float32)
+            for buffer, _ in terms:
+                total = total + buffer[h, g, :, cols].astype(jnp.float32)
+            if final:
+                out_ref[h * half:(h + 1) * half, cols] = total.astype(out_ref.dtype)
+            else:
+                sums[h, g, :, cols] = total.astype(sums.dtype)
+
+    loc, two, one = (from_loc, loc_sem), (from_two, two_sem), (from_one, one_sem)
+    low, high = (from_low, low_sem), (from_high, high_sem)
+
+    def third(step, act):
+        for h in range(2):
+            for dz, cond in me.line(step):
+                for g in (me.at(dz, fx=1, fy=1), me.at(dz, **flips[1 - h])):
+                    act(h, g, cond)
+
+    def second(step, act):
+        for h in range(2):
+            for dz, cond in me.line(step):
+                act(h, me.at(dz, **flips[h]), cond)
+
+    def first(step, act):
+        for h in range(2):
+            for dz, cond in me.line(step):
+                act(h, me.at(dz), cond, dz)
+
+    steps = range(me.deep - 1, -1, -1)
+    for step in steps:
+        third(step, to_core)
+    for step in steps:
+        second(step, to_core)
+        first(step, lambda h, g, cond, dz: to_core(h, g, cond))
+
+    def cross_two(h, g, cond):
+        when(cond, lambda: add(h, g, [loc]))
+        send(cond, h, g, from_two, two_sem, (me.at(**flips[1 - h]), me.c))
+
+    def cross_one(h, g, cond):
+        when(cond, lambda: add(h, g, [loc, two]))
+        send(cond, h, g, from_one, one_sem, (me.at(**flips[h]), me.c))
+
+    def cross_line(h, g, cond, dz):
+        if dz > 0:
+            edge, near, away = me.below, low, me.at(1)
+        elif dz < 0:
+            edge, near, away = me.above, high, me.at(-1)
+        else:
+            for under in (False, True):
+                for over in (False, True):
+                    if me.deep == 1 and (under or over):
+                        continue
+                    fits = jnp.logical_and(me.below == under, me.above == over)
+                    terms = [loc, two, one] + [low] * under + [high] * over
+                    pl.when(fits)(lambda terms=terms: add(h, g, terms, True))
+            return
+        pl.when(jnp.logical_and(cond, edge))(lambda: add(h, g, [loc, two, one, near]))
+        inner = jnp.logical_and(cond, jnp.logical_not(edge))
+        pl.when(inner)(lambda: add(h, g, [loc, two, one]))
+        target = low if dz > 0 else high
+        send(cond, h, g, target[0], target[1], (away, me.c))
+
+    for turn in range(me.deep + 2):
+        for stage, act, lag in ((third, cross_two, 0), (second, cross_one, 1), (first, cross_line, 2)):
+            if 0 <= turn - lag < me.deep:
+                stage(me.deep - 1 - (turn - lag), act)
+    for cond, copy in sends:
+        when(cond, copy.wait_send)
+
+
+def scatter_sums(partial, columns):
+    rows = partial.shape[0] // (2 * columns)
+    width = partial.shape[1]
+    dma = pltpu.SemaphoreType.DMA
+    buffer = pltpu.VMEM((2, columns, rows // 2, width), partial.dtype)
+    return pl.pallas_call(
+        functools.partial(scatter_kernel, columns),
+        out_shape=jax.ShapeDtypeStruct((rows, width), partial.dtype),
+        in_specs=[pl.BlockSpec(memory_space=pltpu.VMEM)],
+        out_specs=pl.BlockSpec(memory_space=pltpu.VMEM),
+        scratch_shapes=[buffer] * 6 + [dma((2, columns))] * 7,
+        compiler_params=pltpu.CompilerParams(
+            collective_id=2, has_side_effects=True, vmem_limit_bytes=48 * 2**20),
+        name="scatter_sums",
+    )(partial)
+
+
+def dense_body(tokens, gate_weights, expert_ids, w_gate, w_up, w_down):
+    width = tokens.shape[1]
+    local_experts = w_gate.shape[0]
+    columns = lax.axis_size("grp")
+    expert_total = columns * local_experts
+    padded = -(-expert_total // LANES) * LANES
+    numbers = jnp.arange(padded, dtype=jnp.int32)
+    chosen = expert_ids[:, :, None] == numbers[None, None, :]
+    table = jnp.sum(
+        jnp.where(chosen, gate_weights.astype(jnp.float32)[:, :, None], 0.0), axis=1
+    ).astype(jnp.bfloat16)
+    gathered = gather_tokens(jnp.concatenate([tokens, table], axis=1), columns)
+    rows = gathered[:, :width]
+    first = width + lax.axis_index("grp") * local_experts
+    scales = lax.dynamic_slice_in_dim(gathered, first, local_experts, axis=1).astype(jnp.float32)
+    hidden = []
+    for expert in range(local_experts):
+        gate_act = jnp.dot(rows, w_gate[expert], preferred_element_type=jnp.float32)
+        upward = jnp.dot(rows, w_up[expert], preferred_element_type=jnp.float32)
+        value = jax.nn.silu(gate_act) * upward * scales[:, expert : expert + 1]
+        hidden.append(value.astype(jnp.bfloat16))
+    partial = None
+    for expert in range(local_experts):
+        term = lax.dot_general(
+            hidden[expert], w_down[expert], (((1,), (1,)), ((), ())),
+            preferred_element_type=jnp.float32,
+        )
+        partial = term if partial is None else partial + term
+    return scatter_sums(partial.astype(jnp.bfloat16), columns)
 
 
 def expert_rows(inputs, scales, gate_part, up_part, down_part):
@@ -54,7 +357,7 @@
     return stacked.astype(jnp.bfloat16)
 
 
-def body(tokens, gate_weights, expert_ids, w_gate, w_up, w_down):
+def slot_body(tokens, gate_weights, expert_ids, w_gate, w_up, w_down):
     tok_count = tokens.shape[0]
     choices_per = expert_ids.shape[1]
     feature_count = tokens.shape[1]
@@ -96,6 +399,16 @@
     return mixed_out.astype(jnp.bfloat16)
 
 
+def body(tokens, gate_weights, expert_ids, w_gate, w_up, w_down):
+    tok_count = tokens.shape[0]
+    columns = lax.axis_size("grp")
+    slot_depth = 2 * tok_count * RGROUPS // (columns * w_gate.shape[0])
+    dense = slot_depth * w_gate.shape[0] >= tok_count
+    fits = columns % 4 == 0 and lax.axis_size("loc") == 2 and tok_count % 32 == 0
+    chosen = dense_body if dense and fits else slot_body
+    return chosen(tokens, gate_weights, expert_ids, w_gate, w_up, w_down)
+
+
 def solution(mesh):
     placed = (
         P(("grp", "loc"), None),

time: 275 us -> 128 us (0.47)
  blocking collectives: 98 us -> 0 us
  Pallas kernels: 0 us -> 82 us
  waiting for transfers between devices: 74.5 us -> 0 us
  local copies, waits for them, and re-layouts: 33.1 us -> 2.71 us
  between operations: 13.3 us -> 0.06 us
  starting transfers between devices: 13 us -> 0 us
    all_to_all x1 -> x0, blocking collectives: 98 us -> none  [body(): lax.all_to_all(computed, 'grp', split_axis=0, concat_axis=0, tiled=True)]
    pallas_call x0 -> x2, Pallas kernels: none -> 82 us  [the longest x1 42.3 us: scatter_sums(): pl.pallas_call(functools.partial(scatter_kernel, columns), out_shape=jax....]
    all_to_all x2 -> x0, waiting for transfers between devices: 72.4 us -> none  [the longest x1 69.3 us: body(): lax.all_to_all(send_rows, 'grp', split_axis=0, concat_axis=0, tiled=True)]
    squeeze x3 -> x0, local copies, waits for them, and re-layouts: 27.4 us -> none  [the longest x1 10.6 us: weights_path(): up_piece[expert][:, lower_unit:upper_unit]]
    all_to_all x2 -> x0, starting transfers between devices: 13 us -> none  [the longest x1 8.34 us: body(): lax.all_to_all(send_scales, 'grp', split_axis=0, concat_axis=0, tiled=True)]
    another operation x3 -> x0, other arithmetic: 3.41 us -> none
    slice x1, local copies, waits for them, and re-layouts: 3.52 us -> 0.5 us  [dense_body(): value = jax.nn.silu(gate_act) * upward * scales[:, expert:expert + 1]]
    dot_general x10 -> x4, matrix products: 39.3 us -> 41.3 us  [the longest x2 32 us: dense_body(): lax.dot_general(hidden[expert], w_down[expert], (((1,), (1,)), ((), ())),...]
  transfers between devices with their start and end apart: 5 -> 0, of which waited for: 2 -> 0; matrix products, arithmetic and copies ran while one was open for 12% -> 0% of each run, Pallas kernels for 0% -> 0%
where the time goes in v1:
time: 128 us; the launch traced here: 127 us
  Pallas kernels  82 us (64%)
  matrix products  41.3 us (32%)
  local copies, waits for them, and re-layouts  2.71 us (2%)
  other arithmetic  1.4 us (1%)
    pallas_call x1, Pallas kernels, scatter_sums(): pl.pallas_call(functools.partial(scatter_kernel, columns), out_shape=jax....  42.3 us
    pallas_call x1, Pallas kernels, gather_tokens(): pl.pallas_call(functools.partial(gather_kernel, columns), out_shape=jax.S...  39.7 us
    dot_general x2, matrix products, dense_body(): lax.dot_general(hidden[expert], w_down[expert], (((1,), (1,)), ((), ())),...  32 us
    dot_general x2, matrix products, dense_body(): gate_act = jnp.dot(rows, w_gate[expert], preferred_element_type=jnp.float32)  9.23 us

profile of v1, /device:TPU:0, one launch (start us, length us, event | category | flops | bytes accessed | tf_op | source)
XLA Modules:
  0.0 127.4 jit_solution(990400664043827064)
XLA Ops:
  0.0 0.8 copy.12
  0.8 0.8 copy.11
  1.5 0.0 copy-start.1
  1.5 0.1 select_reduce_fusion
  1.7 1.1 pad_maximum_fusion.own_ref
  2.8 39.7 %gather_tokens.1 = bf16[1024,3712]{1,0:T(8,128)(2,1)S(1)} custom-call(bf16[32,3712]{1,0:T(8,128)(2,1)S(1)} %pad_maximum_fusion.own_ref), custom_call_target="tpu_custom_call" | custom-call | tf_op jit(solution)/shard_map/gather_tokens/pallas_call | solution.py:143
  42.5 0.0 copy-start
  42.5 0.1 dynamic-slice_convert_fusion
  42.7 0.5 slice_reduce_fusion
  43.2 0.0 copy-done.1
  43.2 3.9 %fusion.2 = f32[1024,512]{1,0:T(8,128)S(1)} fusion(bf16[1024,3712]{1,0:T(8,128)(2,1)S(1)} %gather_tokens.1, bf16[2,3584,512]{2,1,0:T(8,128)(2,1)S(1)} %copy-done.1), kind=kOutput, calls=%fused_computation.3 | convolution fusion | flops 3758096384 | bytes 13107200 | tf_op jit(solution)/shard_map/dot_general | solution.py:298
  47.1 0.0 copy-done
  47.1 5.3 %fusion.6 = f32[1024,512]{1,0:T(8,128)} fusion(bf16[1024,3712]{1,0:T(8,128)(2,1)S(1)} %gather_tokens.1, bf16[2,3584,512]{2,1,0:T(8,128)(2,1)S(1)} %copy-done.1), kind=kOutput, calls=%fused_computation.7 | convolution fusion | flops 3758096384 | bytes 13107200 | tf_op jit(solution)/shard_map/dot_general | solution.py:298
  52.4 15.7 %fusion.11 = f32[1024,3584]{1,0:T(8,128)} fusion(bf16[2,3584,512]{2,1,0:T(8,128)(2,1)} %param.11, f32[1024,512]{1,0:T(8,128)} %fusion.6, bf16[2,3584,512]{2,1,0:T(8,128)(2,1)} %param.10, bf16[1024,3712]{1,0:T(8,128)(2,1)} %copy-done, f32[1024]{0:T(1024)S(1)} %get-tuple-element.6), kind=kOutput, calls=%fused_computation.12 | convolution fusion | flops 7519862784 | bytes 31461376 | tf_op jit(solution)/shard_map/dot_general | solution.py:304
  68.1 16.3 %add_convert_fusion.part_ref = bf16[1024,3584]{1,0:T(8,128)(2,1)} fusion(f32[1024,3584]{1,0:T(8,128)} %fusion.11, bf16[2,3584,512]{2,1,0:T(8,128)(2,1)} %param.11, f32[1024,512]{1,0:T(8,128)S(1)} %fusion.2, bf16[2,3584,512]{2,1,0:T(8,128)(2,1)} %param.10, bf16[1024,3712]{1,0:T(8,128)(2,1)} %copy-done, f32[1024]{0:T(1024)S(1)} %get-tuple-element.5), kind=kOutput, calls=%fused_computation | convolution fusion | flops 7527202816 | bytes 38801408 | tf_op jit(solution)/shard_map/dot_general | solution.py:304
  84.5 42.3 %scatter_sums.1 = bf16[32,3584]{1,0:T(8,128)(2,1)S(1)} custom-call(bf16[1024,3584]{1,0:T(8,128)(2,1)} %add_convert_fusion.part_ref), custom_call_target="tpu_custom_call" | custom-call | tf_op jit(solution)/shard_map/scatter_sums/pallas_call | solution.py:269
  126.8 0.7 copy.14
Async XLA Ops:
  1.5 41.7 %copy-start.1 = (bf16[2,3584,512]{2,1,0:T(8,128)(2,1)S(1)}, bf16[2,3584,512]{2,1,0:T(8,128)(2,1)}, u32[]{:S(2)}) copy-start(bf16[2,3584,512]{2,1,0:T(8,128)(2,1)} %param.9) | copy-start | bytes 22020100
  42.5 4.6 %copy-start = (bf16[1024,3712]{1,0:T(8,128)(2,1)}, bf16[1024,3712]{1,0:T(8,128)(2,1)S(1)}, u32[]{:S(2)}) copy-start(bf16[1024,3712]{1,0:T(8,128)(2,1)S(1)} %gather_tokens.1) | copy-start | bytes 22806532

commit v2 on v1

--- a/solution.py
+++ b/solution.py
@@ -273,9 +273,36 @@
         out_specs=pl.BlockSpec(memory_space=pltpu.VMEM),
         scratch_shapes=[buffer] * 6 + [dma((2, columns))] * 7,
         compiler_params=pltpu.CompilerParams(
-            collective_id=2, has_side_effects=True, vmem_limit_bytes=48 * 2**20),
+            collective_id=2, has_side_effects=True, vmem_limit_bytes=34 * 2**20),
         name="scatter_sums",
     )(partial)
+
+
+def down_kernel(*refs):
+    *hidden, down_ref, out_ref = refs
+    total = None
+    for expert, ref in enumerate(hidden):
+        term = lax.dot_general(
+            ref[...], down_ref[expert], (((1,), (1,)), ((), ())),
+            preferred_element_type=jnp.float32)
+        total = term if total is None else total + term
+    out_ref[...] = total.astype(out_ref.dtype)
+
+
+def project_down(hidden, w_down):
+    experts, width, units = w_down.shape
+    rows = hidden[0].shape[0]
+    tile = 512 if width % 512 == 0 else width
+    return pl.pallas_call(
+        down_kernel,
+        grid=(width // tile,),
+        out_shape=jax.ShapeDtypeStruct((rows, width), jnp.bfloat16),
+        in_specs=[pl.BlockSpec((rows, units), lambda i: (0, 0))] * experts
+        + [pl.BlockSpec((experts, tile, units), lambda i: (0, i, 0))],
+        out_specs=pl.BlockSpec((rows, tile), lambda i: (0, i)),
+        compiler_params=pltpu.CompilerParams(vmem_limit_bytes=24 * 2**20),
+        name="project_down",
+    )(*hidden, w_down)
 
 
 def dense_body(tokens, gate_weights, expert_ids, w_gate, w_up, w_down):
@@ -295,18 +322,13 @@
     scales = lax.dynamic_slice_in_dim(gathered, first, local_experts, axis=1).astype(jnp.float32)
     hidden = []
     for expert in range(local_experts):
-        gate_act = jnp.dot(rows, w_gate[expert], preferred_element_type=jnp.float32)
+        gate_act = lax.optimization_barrier(
+            jnp.dot(rows, w_gate[expert], preferred_element_type=jnp.float32))
         upward = jnp.dot(rows, w_up[expert], preferred_element_type=jnp.float32)
         value = jax.nn.silu(gate_act) * upward * scales[:, expert : expert + 1]
         hidden.append(value.astype(jnp.bfloat16))
-    partial = None
-    for expert in range(local_experts):
-        term = lax.dot_general(
-            hidden[expert], w_down[expert], (((1,), (1,)), ((), ())),
-            preferred_element_type=jnp.float32,
-        )
-        partial = term if partial is None else partial + term
-    return scatter_sums(partial.astype(jnp.bfloat16), columns)
+    partial = project_down(lax.optimization_barrier(tuple(hidden)), w_down)
+    return scatter_sums(partial, columns)
 
 
 def expert_rows(inputs, scales, gate_part, up_part, down_part):

time: 128 us -> 112 us (0.88)
  matrix products: 41.3 us -> 18.5 us
  Pallas kernels: 82 us -> 88.9 us
    dot_general x4, matrix products: 41.3 us -> 18.5 us  [the longest x2 10.6 us: dense_body(): upward = jnp.dot(rows, w_up[expert], preferred_element_type=jnp.float32)]
    pallas_call x0 -> x1, Pallas kernels: none -> 9.9 us  [project_down(): pl.pallas_call(down_kernel, grid=(width // tile,), out_shape=jax.ShapeDty...]
    pallas_call x1, Pallas kernels: 42.3 us -> 39.2 us  [scatter_sums(): pl.pallas_call(functools.partial(scatter_kernel, columns), out_shape=jax....]
where the time goes in v2:
time: 112 us; the launch traced here: 111 us
  Pallas kernels  88.9 us (79%)
  matrix products  18.5 us (17%)
  local copies, waits for them, and re-layouts  2.74 us (2%)
  other arithmetic  1.25 us (1%)
    pallas_call x1, Pallas kernels, gather_tokens(): pl.pallas_call(functools.partial(gather_kernel, columns), out_shape=jax.S...  39.7 us
    pallas_call x1, Pallas kernels, scatter_sums(): pl.pallas_call(functools.partial(scatter_kernel, columns), out_shape=jax....  39.2 us
    dot_general x2, matrix products, dense_body(): upward = jnp.dot(rows, w_up[expert], preferred_element_type=jnp.float32)  10.6 us
    pallas_call x1, Pallas kernels, project_down(): pl.pallas_call(down_kernel, grid=(width // tile,), out_shape=jax.ShapeDty...  9.9 us
    dot_general x2, matrix products, dense_body(): jnp.dot(rows, w_gate[expert], preferred_element_type=jnp.float32)  7.87 us

profile of v2, /device:TPU:0, one launch (start us, length us, event | category | flops | bytes accessed | tf_op | source)
XLA Modules:
  0.0 111.5 jit_solution(14701702670843163688)
XLA Ops:
  0.0 0.8 copy.12
  0.8 0.8 copy.11
  1.5 0.1 select_reduce_fusion
  1.7 1.0 pad_maximum_fusion.own_ref
  2.6 0.0 copy-start
  2.6 39.7 %gather_tokens.1 = bf16[1024,3712]{1,0:T(8,128)(2,1)S(1)} custom-call(bf16[32,3712]{1,0:T(8,128)(2,1)S(1)} %pad_maximum_fusion.own_ref), custom_call_target="tpu_custom_call" | custom-call | tf_op jit(solution)/shard_map/gather_tokens/pallas_call | solution.py:143
  42.4 0.1 dynamic-slice_convert_fusion
  42.5 0.0 slice-start.2
  42.5 0.5 slice_reduce_fusion
  43.0 0.0 copy-done
  43.1 0.0 slice-start.3
  43.1 3.9 %fusion.2 = f32[1024,512]{1,0:T(8,128)S(1)} fusion(bf16[1024,3712]{1,0:T(8,128)(2,1)S(1)} %gather_tokens.1, bf16[2,3584,512]{2,1,0:T(8,128)(2,1)S(1)} %copy-done), kind=kOutput, calls=%fused_computation.2 | convolution fusion | flops 3758096384 | bytes 13107200 | tf_op jit(solution)/shard_map/dot_general | solution.py:326
  47.0 0.0 slice-done.2
  47.0 0.0 slice-done.3
  47.0 4.2 %multiply_convert_fusion.refs_1_ = bf16[1024,512]{1,0:T(8,128)(2,1)S(1)} fusion(f32[1024,512]{1,0:T(8,128)S(1)} %fusion.2, bf16[2,3584,512]{2,1,0:T(8,128)(2,1)S(1)} %bitcast.19, bf16[1024,3712]{1,0:T(8,128)(2,1)S(1)} %gather_tokens.1, f32[1024]{0:T(1024)S(1)} %get-tuple-element.9), kind=kOutput, calls=%fused_computation.16 | convolution fusion | flops 3761766400 | bytes 14159872 | tf_op jit(solution)/shard_map/dot_general | solution.py:327
  51.2 0.0 slice-start
  51.2 3.9 %fusion.6 = f32[1024,512]{1,0:T(8,128)S(1)} fusion(bf16[1024,3712]{1,0:T(8,128)(2,1)S(1)} %gather_tokens.1, bf16[2,3584,512]{2,1,0:T(8,128)(2,1)S(1)} %copy-done), kind=kOutput, calls=%fused_computation.6 | convolution fusion | flops 3758096384 | bytes 13107200 | tf_op jit(solution)/shard_map/dot_general | solution.py:326
  55.2 0.0 slice-start.1
  55.2 6.4 %multiply_convert_fusion.1.refs_0_ = bf16[1024,512]{1,0:T(8,128)(2,1)S(1)} fusion(f32[1024,512]{1,0:T(8,128)S(1)} %fusion.6, bf16[2,3584,512]{2,1,0:T(8,128)(2,1)} %param.10, bf16[1024,3712]{1,0:T(8,128)(2,1)S(1)} %gather_tokens.1, f32[1024]{0:T(1024)S(1)} %get-tuple-element.10), kind=kOutput, calls=%fused_computation.17 | convolution fusion | flops 3761766400 | bytes 14159872 | tf_op jit(solution)/shard_map/dot_general | solution.py:327
  61.6 0.0 slice-done
  61.6 0.0 slice-done.1
  61.6 9.9 %project_down.1.part_ref = bf16[1024,3584]{1,0:T(8,128)(2,1)S(1)} custom-call(bf16[1024,512]{1,0:T(8,128)(2,1)S(1)} %multiply_convert_fusion.1.refs_0_, bf16[1024,512]{1,0:T(8,128)(2,1)S(1)} %multiply_convert_fusion.refs_1_, bf16[2,3584,512]{2,1,0:T(8,128)(2,1)S(1)} %bitcast.17), custom_call_target="tpu_custom_call" | custom-call | tf_op jit(solution)/shard_map/project_down/pallas_call | solution.py:296
  71.5 39.2 %scatter_sums.1 = bf16[32,3584]{1,0:T(8,128)(2,1)S(1)} custom-call(bf16[1024,3584]{1,0:T(8,128)(2,1)S(1)} %project_down.1.part_ref), custom_call_target="tpu_custom_call" | custom-call | tf_op jit(solution)/shard_map/scatter_sums/pallas_call | solution.py:269
  110.8 0.7 copy.14
  (2 shorter events, 0.0 us)
Async XLA Ops:
  2.6 40.4 %copy-start = (bf16[2,3584,512]{2,1,0:T(8,128)(2,1)S(1)}, bf16[2,3584,512]{2,1,0:T(8,128)(2,1)}, u32[]{:S(2)}) copy-start(bf16[2,3584,512]{2,1,0:T(8,128)(2,1)} %param.9) | copy-start | bytes 22020100
  42.5 4.5 %slice-start.2 = ((s8[7340032]{0:T(1024)(128)(4,1)}), s8[4194304]{0:T(1024)(128)(4,1)S(1)}, s32[]{:S(2)}) async-start(s8[7340032]{0:T(1024)(128)(4,1)} %bitcast.18), calls=%async_computation.2 | async-start | bytes 8388608
  43.1 4.0 %slice-start.3 = ((s8[7340032]{0:T(1024)(128)(4,1)}), s8[3145728]{0:T(1024)(128)(4,1)S(1)}, s32[]{:S(2)}) async-start(s8[7340032]{0:T(1024)(128)(4,1)} %bitcast.18), calls=%async_computation.3 | async-start | bytes 6291456
  51.2 10.4 %slice-start = ((s8[7340032]{0:T(1024)(128)(4,1)}), s8[4194304]{0:T(1024)(128)(4,1)S(1)}, s32[]{:S(2)}) async-start(s8[7340032]{0:T(1024)(128)(4,1)} %bitcast.16), calls=%async_computation | async-start | bytes 8388608
  55.2 6.4 %slice-start.1 = ((s8[7340032]{0:T(1024)(128)(4,1)}), s8[3145728]{0:T(1024)(128)(4,1)S(1)}, s32[]{:S(2)}) async-start(s8[7340032]{0:T(1024)(128)(4,1)} %bitcast.16), calls=%async_computation.1 | async-start | bytes 6291456
